TPU v7x, 256 devices: a whole 4x4x8 slice. The times are simulated.
256 devices in a mesh: pgroup: 32 (over y, x, core), tile: 8 (over z).
Axes of the slice: x: 4, y: 4, z: 8, core: 2. Of those that a mesh axis runs over, the one named last changes fastest.
Arguments:
- images: float32 [512, 256, 2048], P(('pgroup', 'tile')), may hold values from -6 to 6
- beams: float32 [512, 256, 2048], P(('pgroup', 'tile')), may hold values from 0.2 to 1
- row_block: int32 [512], P(('pgroup', 'tile')), may hold values from 0 to 30, as said below
- col_block: int32 [512], P(('pgroup', 'tile')), may hold values from 0 to 16
- band: int32 [512, 2], P(('pgroup', 'tile')), may hold values from 0 to 3
- row_frac: float32 [512], P(('pgroup', 'tile')), may hold values from 0.05 to 0.95
- col_frac: float32 [512], P(('pgroup', 'tile')), may hold values from 0.05 to 0.95
Outputs:
- numer: float32 [4096, 4096], P('tile', 'pgroup')
- weight: float32 [4096, 4096], P('tile', 'pgroup')
- normalised: float32 [4096, 4096], P('tile', 'pgroup')
Inputs may be any that keep to these rules, and one draw needn't show every extreme that they name: With t = (p // 2) mod 8, row_block[p] - 4 t lies in 0 to 2, and the largest value is taken in every draw.
All inputs are finite; a program needn't handle non-finite values.
Results may differ from a plain program's by a relative error of at most 0.00002.
Values sent between devices are 32-bit elements; how exact they have to be, the bound alone decides.
A program may use at most 128 MiB of HBM per device.

v0:
```python
import jax
import jax.numpy as jnp
from jax import lax
from jax.sharding import PartitionSpec as P

IMG_BLOCKS = 2
TILE_BLOCKS = 4
SKY_COLS = 4096
HALO = 4


def shifted(block, axis, distance):
    devices = range(lax.axis_size(axis))
    route = [(i - distance, i) for i in devices if i - distance in devices]
    return lax.ppermute(block, axis, route)


def contribution(image_block, beam_block, shift, row_f, col_f, margin):
    stacked = jnp.stack([beam_block * image_block, beam_block * beam_block])
    moved = jnp.concatenate([jnp.zeros_like(stacked[:, :, :1]), stacked[:, :, :-1]], axis=2)
    banded = (1.0 - col_f) * stacked + col_f * moved
    empty = jnp.zeros((2, 128 + margin, banded.shape[2]), jnp.float32)
    zero = jnp.int32(0)
    first = lax.dynamic_update_slice(empty, (1.0 - row_f) * banded, (zero, shift, zero))
    second = lax.dynamic_update_slice(empty, row_f * banded, (zero, shift + 1, zero))
    return first + second


def body(images, beams, row_block, col_block, band, row_frac, col_frac):
    own_rows = TILE_BLOCKS * 128
    canvas = jnp.zeros((2, own_rows + HALO, SKY_COLS), jnp.float32)
    first_block = lax.axis_index("tile") * TILE_BLOCKS
    zero = jnp.int32(0)
    for which in range(images.shape[0]):
        for block in range(IMG_BLOCKS):
            piece = contribution(
                images[which, block * 128 : (block + 1) * 128],
                beams[which, block * 128 : (block + 1) * 128],
                band[which, block],
                row_frac[which],
                col_frac[which],
                HALO,
            )
            row_start = (row_block[which] - first_block + block) * 128
            col_start = col_block[which] * 128
            old = lax.dynamic_slice(canvas, (zero, row_start, col_start), piece.shape)
            canvas = lax.dynamic_update_slice(canvas, old + piece, (zero, row_start, col_start))
    border = shifted(canvas[:, own_rows:], "tile", 1)
    owned = canvas[:, :own_rows].at[:, :HALO].add(border)
    summed = lax.psum_scatter(owned, "pgroup", scatter_dimension=2, tiled=True)
    numer = summed[0]
    weight = summed[1]
    normalised = numer / jnp.maximum(weight, 0.05)
    return (numer, weight, normalised)


def solution(mesh):
    return jax.shard_map(
        body,
        mesh=mesh,
        in_specs=(
            P(("pgroup", "tile"), None, None),
            P(("pgroup", "tile"), None, None),
            P(("pgroup", "tile")),
            P(("pgroup", "tile")),
            P(("pgroup", "tile"), None),
            P(("pgroup", "tile")),
            P(("pgroup", "tile")),
        ),
        out_specs=(P("tile", "pgroup"), P("tile", "pgroup"), P("tile", "pgroup")),
        check_vma=False,
    )
```

profile of v0, /device:TPU:1, one launch (start us, length us, event | category | flops | bytes accessed | tf_op | source)
XLA Modules:
  0.0 354.1 jit_solution(1538355844117940288)
XLA Ops:
  29.0 5.8 %slice_multiply_fusion.4 = (f32[1,128,2048]{2,1,0:T(8,128)}, f32[1,128,2048]{2,1,0:T(8,128)S(1)}, f32[1,128,2048]{2,1,0:T(8,128)S(1)}, f32[1,128,2048]{2,1,0:T(8...) fusion(f32[2,256,2048]{2,1,0:T(8,128)} %param.10, ...), kind=kLoop, calls=%fused_computation.39 | loop fusion | flops 2097152 | bytes 16777216 | tf_op jit(solution)/shard_map/mul | solution.py:19
  43.7 6.7 %dynamic_update_slice.48 = f32[2,132,2048]{2,1,0:T(8,128)} dynamic-update-slice(f32[2,132,2048]{2,1,0:T(8,128)} %broadcast.39.clone.1, f32[2,128,2048]{2,1,0:T(8,128)S(1)} %broadcast_multiply_fusion.2, s32[]{:T(128)} %constant.49.clone.1, s32[]{:T(128)S(6)} %select_n.55, s32[]{:T(128)} %constant.49.clone.1) | dynamic-update-slice | bytes 4194308 | tf_op jit(solution)/shard_map/dynamic_update_slice | solution.py:24
  50.7 5.6 %dynamic_update_slice.44 = f32[2,132,2048]{2,1,0:T(8,128)S(1)} dynamic-update-slice(f32[2,132,2048]{2,1,0:T(8,128)S(1)} %broadcast.39.clone, f32[2,128,2048]{2,1,0:T(8,128)} %broadcast_multiply_fusion.3, s32[]{:T(128)} %constant.49.clone.1, s32[]{:T(128)S(6)} %select_n.50, s32[]{:T(128)} %constant.49.clone.1) | dynamic-update-slice | bytes 4194308 | tf_op jit(solution)/shard_map/dynamic_update_slice | solution.py:24
  56.3 8.9 %multiply_add_fusion.2 = (f32[2,128,2048]{2,1,0:T(8,128)}, f32[2,128,2048]{2,1,0:T(8,128)}) fusion(f32[2,132,2048]{2,1,0:T(8,128)} %dynamic_update_slice.48, s32[]{:T(128)S(6)} %select_n.56, f32[]{:T(128)} %bitcast, f32[2,128,2047]{2,1,0:T(8,128)} %copy-done.3, f32[]{:T(128)} %bitcast.1, f32[1,128,2048]{2,1,0:T(8,128)} %copy-done.7, ...), kind=kLoop, calls=%fused_computation.29 | loop fusion | flops 6291456 | bytes 16775188 | tf_op jit(solution)/shard_map/dynamic_update_slice | solution.py:25
  65.2 5.5 %add.134 = f32[2,132,2048]{2,1,0:T(8,128)S(1)} dynamic-update-slice(f32[2,132,2048]{2,1,0:T(8,128)S(1)} %dynamic_update_slice.44, f32[2,128,2048]{2,1,0:T(8,128)} %get-tuple-element.43, s32[]{:T(128)} %constant.49.clone.1, s32[]{:T(128)S(6)} %select_n.51, s32[]{:T(128)} %constant.49.clone.1) | dynamic-update-slice | bytes 4194308 | tf_op jit(solution)/shard_map/add | solution.py:26
  70.7 7.5 %add.143 = f32[2,132,2048]{2,1,0:T(8,128)} dynamic-update-slice(f32[2,132,2048]{2,1,0:T(8,128)} %dynamic_update_slice.48, f32[2,128,2048]{2,1,0:T(8,128)} %get-tuple-element.42, s32[]{:T(128)} %constant.49.clone.1, s32[]{:T(128)S(6)} %select_n.56, s32[]{:T(128)} %constant.49.clone.1) | dynamic-update-slice | bytes 4194308 | tf_op jit(solution)/shard_map/add | solution.py:26
  85.4 5.5 %dynamic_update_slice.56 = f32[2,132,2048]{2,1,0:T(8,128)S(1)} dynamic-update-slice(f32[2,132,2048]{2,1,0:T(8,128)S(1)} %broadcast.39.clone.3, f32[2,128,2048]{2,1,0:T(8,128)} %broadcast_multiply_fusion, s32[]{:T(128)} %constant.49.clone.1, s32[]{:T(128)S(6)} %select_n.62, s32[]{:T(128)} %constant.49.clone.1) | dynamic-update-slice | bytes 4194308 | tf_op jit(solution)/shard_map/dynamic_update_slice | solution.py:24
  91.0 5.5 %multiply_add_fusion = f32[2,128,2048]{2,1,0:T(8,128)} fusion(f32[2,132,2048]{2,1,0:T(8,128)S(1)} %dynamic_update_slice.56, s32[]{:T(128)S(6)} %select_n.63, f32[]{:T(128)} %bitcast.8, f32[2,128,2047]{2,1,0:T(8,128)} %copy-done.1, f32[]{:T(128)} %bitcast.9, f32[1,128,2048]{2,1,0:T(8,128)} %get-tuple-element.22, f32[1,128,2048]{2,1,0:T(8,128)} %get-tuple-element.29, ...), kind=kLoop, calls=%fused_computation.27 | loop fusion | flops 3145728 | bytes 8387600 | tf_op jit(solution)/shard_map/dynamic_update_slice | solution.py:25
  96.4 5.5 %add.159 = f32[2,132,2048]{2,1,0:T(8,128)S(1)} dynamic-update-slice(f32[2,132,2048]{2,1,0:T(8,128)S(1)} %dynamic_update_slice.56, f32[2,128,2048]{2,1,0:T(8,128)} %multiply_add_fusion, s32[]{:T(128)} %constant.49.clone.1, s32[]{:T(128)S(6)} %select_n.63, s32[]{:T(128)} %constant.49.clone.1) | dynamic-update-slice | bytes 4194308 | tf_op jit(solution)/shard_map/add | solution.py:26
  102.0 4.4 %broadcast_multiply_fusion.1 = f32[2,128,2048]{2,1,0:T(8,128)} fusion(f32[]{:T(128)S(6)} %sub.28, f32[2,128,2047]{2,1,0:T(8,128)} %get-tuple-element.45, f32[]{:T(128)} %bitcast.9, f32[1,128,2048]{2,1,0:T(8,128)S(1)} %get-tuple-element.25, f32[1,128,2048]{2,1,0:T(8,128)} %get-tuple-element.26, f32[]{:T(128)S(6)} %sub.29), kind=kLoop, calls=%fused_computation.34 | loop fusion | flops 2621440 | bytes 6290444 | tf_op jit(solution)/shard_map/mul | solution.py:24
  108.6 7.2 %dynamic_update_slice.52 = f32[2,132,2048]{2,1,0:T(8,128)} dynamic-update-slice(f32[2,132,2048]{2,1,0:T(8,128)} %broadcast.39.clone.2, f32[2,128,2048]{2,1,0:T(8,128)} %broadcast_multiply_fusion.1, s32[]{:T(128)} %constant.49.clone.1, s32[]{:T(128)S(6)} %select_n.59, s32[]{:T(128)} %constant.49.clone.1) | dynamic-update-slice | bytes 4194308 | tf_op jit(solution)/shard_map/dynamic_update_slice | solution.py:24
  115.8 5.8 %multiply_add_fusion.1 = f32[2,128,2048]{2,1,0:T(8,128)} fusion(f32[2,132,2048]{2,1,0:T(8,128)} %dynamic_update_slice.52, s32[]{:T(128)S(6)} %select_n.60, f32[]{:T(128)} %bitcast.8, f32[2,128,2047]{2,1,0:T(8,128)} %get-tuple-element.45, f32[]{:T(128)} %bitcast.9, f32[1,128,2048]{2,1,0:T(8,128)S(1)} %get-tuple-element.25, ...), kind=kLoop, calls=%fused_computation.28 | loop fusion | flops 3145728 | bytes 8387600 | tf_op jit(solution)/shard_map/dynamic_update_slice | solution.py:25
  121.6 7.2 %add.151 = f32[2,132,2048]{2,1,0:T(8,128)} dynamic-update-slice(f32[2,132,2048]{2,1,0:T(8,128)} %dynamic_update_slice.52, f32[2,128,2048]{2,1,0:T(8,128)} %multiply_add_fusion.1, s32[]{:T(128)} %constant.49.clone.1, s32[]{:T(128)S(6)} %select_n.60, s32[]{:T(128)} %constant.49.clone.1) | dynamic-update-slice | bytes 4194308 | tf_op jit(solution)/shard_map/add | solution.py:26
  128.8 8.0 %broadcast_in_dim.3 = f32[2,516,4096]{2,1,0:T(8,128)} broadcast(f32[]{:T(128)} %constant.47.clone.1), dimensions={} | broadcast | bytes 16908292 | tf_op jit(solution)/shard_map/broadcast_in_dim | solution.py:31
  136.8 13.5 %dynamic_update_slice.47 = f32[2,516,4096]{2,1,0:T(8,128)} dynamic-update-slice(f32[2,516,4096]{2,1,0:T(8,128)} %broadcast_in_dim.3, f32[2,132,2048]{2,1,0:T(8,128)} %copy-done, s32[]{:T(128)} %constant.49.clone.1, s32[]{:T(128)S(6)} %select_n.52, s32[]{:T(128)S(6)} %select_n.53) | dynamic-update-slice | bytes 4325380 | tf_op jit(solution)/shard_map/dynamic_update_slice | solution.py:47
  150.3 4.4 %dynamic-slice_add_fusion.2 = f32[2,132,2048]{2,1,0:T(8,128)} fusion(f32[2,132,2048]{2,1,0:T(8,128)} %add.143, f32[2,516,4096]{2,1,0:T(8,128)} %dynamic_update_slice.47, s32[]{:T(128)S(6)} %select_n.54, s32[]{:T(128)S(6)} %select_n.53), kind=kLoop, calls=%fused_computation.14 | loop fusion | flops 540672 | bytes 6488072 | tf_op jit(solution)/shard_map/add | solution.py:47
  154.7 13.6 %dynamic_update_slice.51 = f32[2,516,4096]{2,1,0:T(8,128)} dynamic-update-slice(f32[2,516,4096]{2,1,0:T(8,128)} %dynamic_update_slice.47, f32[2,132,2048]{2,1,0:T(8,128)} %dynamic-slice_add_fusion.2, s32[]{:T(128)} %constant.49.clone.1, s32[]{:T(128)S(6)} %select_n.54, s32[]{:T(128)S(6)} %select_n.53) | dynamic-update-slice | bytes 4325380 | tf_op jit(solution)/shard_map/dynamic_update_slice | solution.py:47
  168.3 4.4 %dynamic-slice_add_fusion.1 = f32[2,132,2048]{2,1,0:T(8,128)} fusion(f32[2,132,2048]{2,1,0:T(8,128)} %add.151, f32[2,516,4096]{2,1,0:T(8,128)} %dynamic_update_slice.51, s32[]{:T(128)S(6)} %select_n.57, s32[]{:T(128)S(6)} %select_n.58), kind=kLoop, calls=%fused_computation.13 | loop fusion | flops 540672 | bytes 6488072 | tf_op jit(solution)/shard_map/add | solution.py:47
  172.7 13.2 %dynamic_update_slice.55 = f32[2,516,4096]{2,1,0:T(8,128)} dynamic-update-slice(f32[2,516,4096]{2,1,0:T(8,128)} %dynamic_update_slice.51, f32[2,132,2048]{2,1,0:T(8,128)} %dynamic-slice_add_fusion.1, s32[]{:T(128)} %constant.49.clone.1, s32[]{:T(128)S(6)} %select_n.57, s32[]{:T(128)S(6)} %select_n.58) | dynamic-update-slice | bytes 4325380 | tf_op jit(solution)/shard_map/dynamic_update_slice | solution.py:47
  185.8 3.7 %dynamic-slice_add_fusion = f32[2,132,2048]{2,1,0:T(8,128)} fusion(f32[2,132,2048]{2,1,0:T(8,128)S(1)} %add.159, f32[2,516,4096]{2,1,0:T(8,128)} %dynamic_update_slice.55, s32[]{:T(128)S(6)} %select_n.61, s32[]{:T(128)S(6)} %select_n.58), kind=kLoop, calls=%fused_computation.12 | loop fusion | flops 540672 | bytes 6488072 | tf_op jit(solution)/shard_map/add | solution.py:47
  189.5 12.9 %dynamic_update_slice.59 = f32[2,516,4096]{2,1,0:T(8,128)} dynamic-update-slice(f32[2,516,4096]{2,1,0:T(8,128)} %dynamic_update_slice.55, f32[2,132,2048]{2,1,0:T(8,128)} %dynamic-slice_add_fusion, s32[]{:T(128)} %constant.49.clone.1, s32[]{:T(128)S(6)} %select_n.61, s32[]{:T(128)S(6)} %select_n.58) | dynamic-update-slice | bytes 4325380 | tf_op jit(solution)/shard_map/dynamic_update_slice | solution.py:47
  203.4 5.1 %collective-permute-start = (f32[2,4,4096]{2,1,0:T(4,128)S(1)}, f32[2,4,4096]{2,1,0:T(4,128)S(1)}, u32[]{:S(2)}, u32[]{:S(2)}) collective-permute-start(f32[2,4,4096]{2,1,0:T(4,128)S(1)} %slice.156), channel_id=1, source_target_pairs={{0,1},{1,2},{2,3},{3,4},{4,5},{5,6},{6,7},{8,9},{9,10},{10,11},{11... | collective-permute-start | bytes 393224 | tf_op jit(solution)/shard_map/ppermute | solution.py:15
  208.4 11.6 %slice.154 = f32[2,512,4096]{2,1,0:T(8,128)} slice(f32[2,516,4096]{2,1,0:T(8,128)} %dynamic_update_slice.59), slice={[0:2], [0:512], [0:4096]} | slice | bytes 33554432 | tf_op jit(solution)/shard_map/slice | solution.py:49
  221.7 123.6 %reduce-scatter.2.cloned.1.call-done = f32[2,512,128]{2,1,0:T(8,128)} async-done(((f32[2,512,4096]{2,1,0:T(8,128)}), f32[2,512,128]{2,1,0:T(8,128)}) %reduce-scatter.2.cloned.1.call-update) | async-done | bytes 524304 | tf_op jit(solution)/shard_map/reduce_scatter | solution.py:50
  (41 shorter events, 27.3 us)
Async XLA Ops:
  7.2 338.2 %reduce-scatter.2.cloned.1.call-start = ((), (), s32[]{:S(2)}) async-start(), calls=%async_computation.1 | async-start | bytes 17301504 | tf_op jit(solution)/shard_map/reduce_scatter | solution.py:50
  34.8 1.0 copy-start.7
  34.8 1.3 copy-start.9
  34.8 2.6 copy-start.6
  34.8 2.6 copy-start.8
  35.0 2.5 copy-start.2
  36.1 2.0 copy-start.3
  70.7 7.5 %copy-start = (f32[2,132,2048]{2,1,0:T(8,128)}, f32[2,132,2048]{2,1,0:T(8,128)S(1)}, u32[]{:S(2)}) copy-start(f32[2,132,2048]{2,1,0:T(8,128)S(1)} %add.134) | copy-start | bytes 6488068
  78.9 3.7 %copy-start.4 = (f32[1,128,2048]{2,1,0:T(8,128)S(1)}, f32[1,128,2048]{2,1,0:T(8,128)}, u32[]{:S(2)}) copy-start(f32[1,128,2048]{2,1,0:T(8,128)} %get-tuple-element.22) | copy-start | bytes 3145732
  78.9 3.7 %copy-start.5 = (f32[1,128,2048]{2,1,0:T(8,128)S(1)}, f32[1,128,2048]{2,1,0:T(8,128)}, u32[]{:S(2)}) copy-start(f32[1,128,2048]{2,1,0:T(8,128)} %get-tuple-element.29) | copy-start | bytes 3145732
  82.6 2.6 copy-start.1
  203.4 16.6 %collective-permute-start = (f32[2,4,4096]{2,1,0:T(4,128)S(1)}, f32[2,4,4096]{2,1,0:T(4,128)S(1)}, u32[]{:S(2)}, u32[]{:S(2)}) collective-permute-start(f32[2,4,4096]{2,1,0:T(4,128)S(1)} %slice.156), channel_id=1, source_target_pairs={{0,1},{1,2},{2,3},{3,4},{4,5},{5,6},{6,7},{8,9},{9,10},{10,11},{11... | collective-permute-start | bytes 393224 | tf_op jit(solution)/shard_map/ppermute | solution.py:15
Sparse Core Ops, SparseCore 0:
  221.8 123.4 reduce-scatter.1
where the time goes:
time: 358 us; the launch traced here: 354 us
  local copies, waits for them, and re-layouts  137 us (38%)
  waiting for transfers between devices  124 us (35%)
  other arithmetic  57 us (16%)
  between operations  31.7 us (9%)
  starting transfers between devices  5.1 us (1%)
    reduce_scatter x1, waiting for transfers between devices, body(): summed = lax.psum_scatter(owned, 'pgroup', scatter_dimension=2, tiled=True)  124 us
    dynamic_update_slice x4, local copies, waits for them, and re-layouts, body(): lax.dynamic_update_slice(canvas, old + piece, (zero, row_start, col_start))  53.2 us
    add x4, local copies, waits for them, and re-layouts, contribution(): return first + second  25.8 us
    dynamic_update_slice x4, local copies, waits for them, and re-layouts, contribution(): lax.dynamic_update_slice(empty, (1.0 - row_f) * banded, (zero, shift, zero))  25 us
    dynamic_update_slice x3, other arithmetic, contribution(): lax.dynamic_update_slice(empty, row_f * banded, (zero, shift + 1, zero))  20.2 us
    add x3, other arithmetic, body(): old + piece  12.4 us
    slice x1, local copies, waits for them, and re-layouts, body(): owned = canvas[:, :own_rows].at[:, :HALO].add(border)  11.6 us
    mul x4, other arithmetic, contribution(): (1.0 - row_f) * banded  11 us
  transfers between devices with their start and end apart: 2, of which 1 were waited for; matrix products, arithmetic and copies ran while one was open for 3% of the time, Pallas kernels for 0%

commit v1 on v0

v1 whole, which is shorter than its diff:
```python
import jax
import jax.numpy as jnp
from jax import lax
from jax.experimental import pallas as pl
from jax.experimental.pallas import tpu as pltpu
from jax.sharding import PartitionSpec as P

MESH = pl.DeviceIdType.MESH
STRIPS = 16
ROWS = 64
CHUNKS = 8
SKY = 512
LAG = 1


def kernel(
    images, beams, row_block, col_block, band, row_frac, col_frac,
    numer, weight, normalised,
    inp, cols, ra, rb, rc, ta, tb, tc, canvas, hal, hin,
    got_a, got_b, got_c, got_d, got_e, out, their_row, their_col,
    in_sem, par_send, par_recv, strip_send, strip_recv, hal_send, hal_recv,
    send_sem, recv_sem, out_sem,
):
    me = lax.axis_index("pgroup")
    tile = lax.axis_index("tile")
    core = lax.rem(me, 2)
    x = lax.rem(lax.div(me, 2), 4)
    y = lax.div(me, 8)
    partner = me + 1 - 2 * core
    su, sv = 2 + 6 * core, 8 - 6 * core
    u = x + (y - x) * core
    v = y + (x - y) * core
    up = lax.rem(u + 1, 4) * su + v * sv + core
    um = lax.rem(u + 3, 4) * su + v * sv + core
    vp = u * su + lax.rem(v + 1, 4) * sv + core
    vm = u * su + lax.rem(v + 3, 4) * sv + core
    zp, zm = lax.rem(tile + 1, 8), lax.rem(tile + 7, 8)

    def load(p, b, q):
        rows = pl.ds(128 * b, 128)
        source = (images, beams)[q]
        return pltpu.make_async_copy(source.at[p, rows, :], inp.at[p, q, rows, :], in_sem.at[p, b, q])

    for b in range(2):
        for p in range(2):
            for q in range(2):
                load(p, b, q).start()

    barrier = pltpu.get_barrier_semaphore()
    for other in (partner, up, um, vp, vm):
        pl.semaphore_signal(barrier, inc=1, device_id={"pgroup": other, "tile": tile}, device_id_type=MESH)
    for other in (zp, zm):
        pl.semaphore_signal(barrier, inc=1, device_id={"pgroup": me, "tile": other}, device_id_type=MESH)

    def to(src, dst, ssem, rsem, pgroup, z=None):
        return pltpu.make_async_remote_copy(
            src_ref=src, dst_ref=dst, send_sem=ssem, recv_sem=rsem,
            device_id={"pgroup": pgroup, "tile": tile if z is None else z}, device_id_type=MESH,
        )

    edge = jnp.zeros((STRIPS, 8, 128), jnp.float32)
    for p in range(2):
        for b in range(2):
            for q in range(2):
                cols[p, b, q, :, pl.ds(0, 8), :] = edge
                cols[p, b, q, :, pl.ds(136, 8), :] = edge
    for p in range(4):
        ra[p, STRIPS] = jnp.zeros((128, 128), jnp.float32)
        rb[p, STRIPS] = jnp.zeros((128, 128), jnp.float32)
        rc[p, STRIPS] = jnp.zeros((8, 128), jnp.float32)

    @pl.when(tile == 0)
    def _():
        hin[...] = jnp.zeros(hin.shape, jnp.float32)

    pl.semaphore_wait(barrier, 7)

    params = [
        to(row_block, their_row, par_send.at[0], par_recv.at[0], partner),
        to(col_block, their_col, par_send.at[1], par_recv.at[1], partner),
    ]
    for copy in params:
        copy.start()

    first = lax.broadcasted_iota(jnp.int32, (8, 128), 1) == 0

    def band_columns(p, b):
        g = col_frac[p]
        load(p, b, 0).wait()
        load(p, b, 1).wait()

        def step(t, carry):
            rows = pl.ds(pl.multiple_of(128 * b + 8 * t, 8), 8)
            below = pl.ds(pl.multiple_of(8 * t + 8, 8), 8)
            before = [jnp.zeros((8, 128), jnp.float32)] * 2
            for k in range(STRIPS):
                lanes = pl.ds(128 * k, 128)
                beam = inp[p, 1, rows, lanes]
                for q in range(2):
                    value = beam * inp[p, core if q == 0 else 1 - core, rows, lanes]
                    rolled = pltpu.roll(value, 1, 1)
                    moved = jnp.where(first, before[q], rolled)
                    before[q] = rolled
                    cols[p, b, q, k, below, :] = (1.0 - g) * value + g * moved
            return carry

        lax.fori_loop(0, 16, step, 0)

    def mix(p, b, q, k, start, length):
        f = row_frac[p]
        s = band[p, b]
        near = cols[p, b, q, k, pl.ds(start + 8 - s, length), :]
        far = cols[p, b, q, k, pl.ds(start + 7 - s, length), :]
        return (1.0 - f) * near + f * far

    def band_rows_a(p):
        def step(k, carry):
            ta[p, k] = mix(p, 0, 1, k, 0, 128)
            ra[p, k] = mix(p, 0, 0, k, 0, 128)
            return carry

        lax.fori_loop(0, STRIPS, step, 0)

    def band_rows_b(p):
        def step(k, carry):
            for q, (mid, low) in ((1, (tb, tc)), (0, (rb, rc))):
                body = mix(p, 1, q, k, 0, 128)
                mid[p, k, pl.ds(0, 8), :] = body[0:8] + mix(p, 0, q, k, 128, 8)
                mid[p, k, pl.ds(8, 120), :] = body[8:128]
                low[p, k] = mix(p, 1, q, k, 128, 8)
            return carry

        lax.fori_loop(0, STRIPS, step, 0)

    def strips(p, n):
        mine, theirs = ((ta, ra), (tb, rb), (tc, rc))[n]
        return to(mine.at[p], theirs.at[2 + p, pl.ds(0, STRIPS)], strip_send.at[p, n], strip_recv.at[p, n], partner)

    for p in range(2):
        band_columns(p, 0)
        band_rows_a(p)
        strips(p, 0).start()
    for p in range(2):
        band_columns(p, 1)
        band_rows_b(p)
        strips(p, 1).start()
        strips(p, 2).start()

    for copy in params:
        copy.wait()
    offs = [row_block[p] - 4 * tile for p in range(2)] + [their_row[p] - 4 * tile for p in range(2)]
    shifts = [col_block[p] for p in range(2)] + [their_col[p] for p in range(2)]

    def column_of(rel, c):
        return lax.rem(u + rel, 4) * su + lax.rem(v + lax.div(c, 2), 4) * sv + lax.rem(c, 2)

    def generate(k, rel, early):
        turn = lax.rem(k + 1, CHUNKS)
        block = lax.div(turn, 2)
        half = pl.multiple_of(lax.rem(turn, 2) * ROWS, ROWS)
        start = lax.rem(turn, 2) == 0

        def step(c, carry):
            j = column_of(rel, c)
            total = None
            extra = None
            for p in range(4):
                k_in = j - shifts[p]
                inside = (k_in >= 0) & (k_in < STRIPS)
                ia = jnp.where(inside & (block == offs[p]), k_in, STRIPS)
                part = ra[p, ia, pl.ds(half, ROWS), :]
                total = part if total is None else total + part
                if not early:
                    ib = jnp.where(inside & (block == offs[p] + 1), k_in, STRIPS)
                    total = total + rb[p, ib, pl.ds(half, ROWS), :]
                    ic = jnp.where(inside & start & (block == offs[p] + 2), k_in, STRIPS)
                    tail = rc[p, ic]
                    extra = tail if extra is None else extra + tail
            if early:
                canvas[rel, k, c] = total
            else:
                canvas[rel, k, c, pl.ds(0, 8), :] = total[0:8] + extra
                canvas[rel, k, c, pl.ds(8, ROWS - 8), :] = total[8:ROWS]
            return carry

        lax.fori_loop(0, 8, step, 0)

    def border(k, rel):
        @pl.when(k == CHUNKS - 1)
        def _():
            canvas[rel, k, :, pl.ds(0, 8), :] = canvas[rel, k, :, pl.ds(0, 8), :] + hin[rel]

    def copy_a(k, d):
        return to(canvas.at[2, k, pl.ds(4 * d, 4)], got_a.at[d, k], send_sem.at[0, d, k], recv_sem.at[0, d, k], (up, um)[d])

    def copy_b(k, d):
        return to(canvas.at[1 + 2 * d, k], got_b.at[d, k], send_sem.at[1, d, k], recv_sem.at[1, d, k], (up, um)[d])

    def copy_c(k, d):
        return to(canvas.at[0, k, 4 + d], got_c.at[d, k], send_sem.at[2, d, k], recv_sem.at[2, d, k], (vp, vm)[d])

    def copy_d(k, d):
        return to(canvas.at[0, k, pl.ds(2 + 4 * d, 2)], got_d.at[d, k], send_sem.at[3, d, k], recv_sem.at[3, d, k], (vp, vm)[d])

    def copy_e(k):
        return to(canvas.at[0, k, 1 - core], got_e.at[k], send_sem.at[4, 0, k], recv_sem.at[4, 0, k], partner)

    def first_row(k):
        return pl.multiple_of(lax.rem(k + 1, CHUNKS) * ROWS, ROWS)

    def copy_out(k, n):
        rows = pl.ds(first_row(k), ROWS)
        return pltpu.make_async_copy(out.at[n, rows, :], (numer, weight, normalised)[n].at[rows, :], out_sem.at[n, k])

    strips(0, 0).wait_recv()
    strips(1, 0).wait_recv()
    generate(jnp.int32(0), 2, True)
    copy_a(0, 0).start()
    copy_a(0, 1).start()
    for rel in (1, 3, 0):
        generate(jnp.int32(0), rel, True)

    for n in (1, 2):
        for p in range(2):
            strips(p, n).wait_recv()

    halo = to(hal, hin, hal_send, hal_recv, me, zp)

    @pl.when(tile < 7)
    def _():
        def step(n, carry):
            j = column_of(lax.div(n, 8), lax.rem(n, 8))
            total = None
            for p in range(4):
                k_in = j - shifts[p]
                ic = jnp.where((k_in >= 0) & (k_in < STRIPS) & (offs[p] == 2), k_in, STRIPS)
                tail = rc[p, ic]
                total = tail if total is None else total + tail
            hal[lax.div(n, 8), lax.rem(n, 8)] = total
            return carry

        lax.fori_loop(0, 32, step, 0)
        halo.start()

    def iteration(i, carry):
        @pl.when(i < CHUNKS)
        def _():
            @pl.when((i == CHUNKS - 1) & (tile > 0))
            def _():
                halo.wait_recv()

            generate(i, 2, False)
            border(i, 2)
            copy_a(i, 0).start()
            copy_a(i, 1).start()
            for rel in (1, 3, 0):
                generate(i, rel, False)
                border(i, rel)

        kb = i - LAG

        @pl.when((kb >= 0) & (kb < CHUNKS))
        def _():
            for d in range(2):
                copy_a(kb, d).wait_recv()
                part = pl.ds(4 * d, 4)
                canvas[1 + 2 * d, kb, part] = canvas[1 + 2 * d, kb, part] + got_a[d, kb]
                copy_b(kb, d).start()

        kc = i - LAG - 1

        @pl.when((kc >= 0) & (kc < CHUNKS))
        def _():
            copy_b(kc, 0).wait_recv()
            copy_b(kc, 1).wait_recv()
            canvas[0, kc, pl.ds(4, 2)] = canvas[0, kc, pl.ds(4, 2)] + (got_b[0, kc, pl.ds(4, 2)] + got_b[1, kc, pl.ds(4, 2)])
            copy_c(kc, 0).start()
            copy_c(kc, 1).start()
            for part in (pl.ds(0, 4), pl.ds(6, 2)):
                canvas[0, kc, part] = canvas[0, kc, part] + (got_b[0, kc, part] + got_b[1, kc, part])

        kd = i - LAG - 2

        @pl.when((kd >= 0) & (kd < CHUNKS))
        def _():
            for d in range(2):
                copy_c(kd, d).wait_recv()
                spot = 2 + 5 * d
                canvas[0, kd, spot] = canvas[0, kd, spot] + got_c[d, kd]
                copy_d(kd, d).start()

        ke = i - LAG - 3

        @pl.when((ke >= 0) & (ke < CHUNKS))
        def _():
            copy_d(ke, 0).wait_recv()
            copy_d(ke, 1).wait_recv()
            canvas[0, ke, pl.ds(0, 2)] = canvas[0, ke, pl.ds(0, 2)] + (got_d[0, ke] + got_d[1, ke])
            copy_e(ke).start()

        kf = i - LAG - 4

        @pl.when(kf >= 0)
        def _():
            copy_e(kf).wait_recv()
            own = canvas[0, kf, core]
            got = got_e[kf]
            top = jnp.where(core == 0, own, got)
            low = jnp.where(core == 0, got, own)
            rows = pl.ds(first_row(kf), ROWS)
            out[0, rows, :] = top
            out[1, rows, :] = low
            out[2, rows, :] = top / jnp.maximum(low, 0.05)
            for n in range(3):
                copy_out(kf, n).start()

        return carry

    lax.fori_loop(1, CHUNKS + LAG + 4, iteration, 0)

    for copy in [strips(p, n) for p in range(2) for n in range(3)]:
        copy.wait_send()

    @pl.when(tile < 7)
    def _():
        halo.wait_send()

    def finish(k, carry):
        for d in range(2):
            for copy in (copy_a, copy_b, copy_c, copy_d):
                copy(k, d).wait_send()
        copy_e(k).wait_send()
        for n in range(3):
            copy_out(k, n).wait()
        return carry

    lax.fori_loop(0, CHUNKS, finish, 0)


def body(images, beams, row_block, col_block, band, row_frac, col_frac):
    f32 = jnp.float32
    vmem = lambda *shape: pltpu.VMEM(shape, f32)
    dma = pltpu.SemaphoreType.DMA
    piece = jax.ShapeDtypeStruct((SKY, 128), f32)
    hbm = pl.BlockSpec(memory_space=pl.ANY)
    smem = pl.BlockSpec(memory_space=pltpu.SMEM)
    return pl.pallas_call(
        kernel,
        out_shape=(piece, piece, piece),
        in_specs=[hbm, hbm, smem, smem, smem, smem, smem],
        out_specs=(hbm, hbm, hbm),
        scratch_shapes=[
            vmem(2, 2, 256, 2048),
            vmem(2, 2, 2, STRIPS, 144, 128),
            vmem(4, STRIPS + 1, 128, 128),
            vmem(4, STRIPS + 1, 128, 128),
            vmem(4, STRIPS + 1, 8, 128),
            vmem(2, STRIPS, 128, 128),
            vmem(2, STRIPS, 128, 128),
            vmem(2, STRIPS, 8, 128),
            vmem(4, CHUNKS, 8, ROWS, 128),
            vmem(4, 8, 8, 128),
            vmem(4, 8, 8, 128),
            vmem(2, CHUNKS, 4, ROWS, 128),
            vmem(2, CHUNKS, 8, ROWS, 128),
            vmem(2, CHUNKS, ROWS, 128),
            vmem(2, CHUNKS, 2, ROWS, 128),
            vmem(CHUNKS, ROWS, 128),
            vmem(3, SKY, 128),
            pltpu.SMEM((2,), jnp.int32),
            pltpu.SMEM((2,), jnp.int32),
            dma((2, 2, 2)),
            dma((2,)),
            dma((2,)),
            dma((2, 3)),
            dma((2, 3)),
            dma,
            dma,
            dma((5, 2, CHUNKS)),
            dma((5, 2, CHUNKS)),
            dma((3, CHUNKS)),
        ],
        compiler_params=pltpu.CompilerParams(
            collective_id=0, has_side_effects=True, vmem_limit_bytes=66_000_000
        ),
    )(images, beams, row_block, col_block, band, row_frac, col_frac)


def solution(mesh):
    return jax.shard_map(
        body,
        mesh=mesh,
        in_specs=(
            P(("pgroup", "tile"), None, None),
            P(("pgroup", "tile"), None, None),
            P(("pgroup", "tile")),
            P(("pgroup", "tile")),
            P(("pgroup", "tile"), None),
            P(("pgroup", "tile")),
            P(("pgroup", "tile")),
        ),
        out_specs=(P("tile", "pgroup"), P("tile", "pgroup"), P("tile", "pgroup")),
        check_vma=False,
    )
```

time: 358 us -> 79.6 us (0.22); the launches traced: 354 us -> 79.4 us
  local copies, waits for them, and re-layouts: 137 us -> 5.01 us
  waiting for transfers between devices: 124 us -> 0 us
  Pallas kernels: 0 us -> 73.7 us
  other arithmetic: 57 us -> 0 us
  between operations: 31.7 us -> 0.64 us
  starting transfers between devices: 5.1 us -> 0 us
    reduce_scatter x1 -> x0, waiting for transfers between devices: 124 us -> none  [body(): summed = lax.psum_scatter(owned, 'pgroup', scatter_dimension=2, tiled=True)]
    dynamic_update_slice x8 -> x0, local copies, waits for them, and re-layouts: 78.2 us -> none  [the longest x4 53.2 us: body(): lax.dynamic_update_slice(canvas, old + piece, (zero, row_start, col_start))]
    pallas_call x0 -> x1, Pallas kernels: none -> 73.7 us  [body(): pl.pallas_call(kernel, out_shape=(piece, piece, piece), in_specs=[hbm, hb...]
    add x4 -> x0, local copies, waits for them, and re-layouts: 25.8 us -> none  [contribution(): return first + second]
    dynamic_update_slice x3 -> x0, other arithmetic: 20.2 us -> none  [contribution(): lax.dynamic_update_slice(empty, row_f * banded, (zero, shift + 1, zero))]
    slice x7 -> x0, local copies, waits for them, and re-layouts: 19.3 us -> none  [the longest x1 11.6 us: body(): owned = canvas[:, :own_rows].at[:, :HALO].add(border)]
    mul x5 -> x0, other arithmetic: 16.8 us -> none  [the longest x4 11 us: contribution(): (1.0 - row_f) * banded]
    add x3 -> x0, other arithmetic: 12.4 us -> none  [body(): old + piece]
  transfers between devices with their start and end apart: 2 -> 0, of which waited for: 1 -> 0; matrix products, arithmetic and copies ran while one was open for 3% -> 0% of each run, Pallas kernels for 0% -> 0%
where the time goes in v1:
time: 79.6 us; the launch traced here: 79.4 us
  Pallas kernels  73.7 us (93%)
  local copies, waits for them, and re-layouts  5.01 us (6%)
    pallas_call x1, Pallas kernels, body(): pl.pallas_call(kernel, out_shape=(piece, piece, piece), in_specs=[hbm, hb...  73.7 us
    unnamed x3, local copies, waits for them, and re-layouts  5.01 us

profile of v1, /device:TPU:1, one launch (start us, length us, event | category | flops | bytes accessed | tf_op | source)
XLA Modules:
  0.0 79.4 jit_solution(3462893924156328504)
XLA Ops:
  0.6 73.7 %shard_map.94 = (f32[512,128]{1,0:T(8,128)}, f32[512,128]{1,0:T(8,128)}, f32[512,128]{1,0:T(8,128)}) custom-call(f32[2,256,2048]{2,1,0:T(8,128)} %images.1, f32[2,256,2048]{2,1,0:T(8,128)} %beams.1, s32[2]{0:T(128)} %row_block.1, s32[2]{0:T(128)} %col_block.1, s32[2,2]{1,0:T(2,128)} %band.1, f32[2]{0:T(128)} %row_frac.1, f32[2]{0:T(128)} %col_frac.1), custom_call_target="tpu_custom_call" | custom-call | tf_op jit(solution)/shard_map/pallas_call | solution.py:347
  74.4 1.7 %copy.13 = f32[512,128]{1,0:T(8,128)} copy(f32[512,128]{1,0:T(8,128)} %get-tuple-element.6) | data formatting | bytes 524288
  76.1 1.7 %copy.14 = f32[512,128]{1,0:T(8,128)} copy(f32[512,128]{1,0:T(8,128)} %get-tuple-element.7) | data formatting | bytes 524288
  77.7 1.7 %copy.15 = f32[512,128]{1,0:T(8,128)} copy(f32[512,128]{1,0:T(8,128)} %get-tuple-element.8) | data formatting | bytes 524288

commit v2 on v1

v2 whole, which is shorter than its diff:
```python
import jax
import jax.numpy as jnp
from jax import lax
from jax.experimental import pallas as pl
from jax.experimental.pallas import tpu as pltpu
from jax.sharding import PartitionSpec as P

MESH = pl.DeviceIdType.MESH
STRIPS = 16
ROWS = 64
PARTS = 128 // ROWS
CHUNKS = 4 * PARTS
SKY = 512
SLOTS = 4
LAG_B, LAG_C, LAG_D, LAG_F = 1, 2, 3, 4


def kernel(
    images, beams, row_block, col_block, band, row_frac, col_frac,
    numer, weight, normalised,
    inp, cols, ra, rb, rc, ta, tb, tc, canvas, hal, hin,
    got_a, got_b, got_c, got_d, their_row, their_col,
    in_sem, par_send, par_recv, strip_send, strip_recv, hal_send, hal_recv,
    send_sem, recv_sem, last_recv,
):
    me = lax.axis_index("pgroup")
    tile = lax.axis_index("tile")
    core = lax.rem(me, 2)
    x = lax.rem(lax.div(me, 2), 4)
    y = lax.div(me, 8)
    partner = me + 1 - 2 * core
    su, sv = 2 + 6 * core, 8 - 6 * core
    u = x + (y - x) * core
    v = y + (x - y) * core
    up = lax.rem(u + 1, 4) * su + v * sv + core
    um = lax.rem(u + 3, 4) * su + v * sv + core
    vp = u * su + lax.rem(v + 1, 4) * sv + core
    vm = u * su + lax.rem(v + 3, 4) * sv + core
    zp, zm = lax.rem(tile + 1, 8), lax.rem(tile + 7, 8)

    barrier = pltpu.get_barrier_semaphore()
    for chip in (up - core, um - core, vp - core, vm - core):
        for other in (chip, chip + 1):
            pl.semaphore_signal(barrier, inc=1, device_id={"pgroup": other, "tile": tile}, device_id_type=MESH)
    pl.semaphore_signal(barrier, inc=1, device_id={"pgroup": partner, "tile": tile}, device_id_type=MESH)
    for other in (zp, zm):
        pl.semaphore_signal(barrier, inc=1, device_id={"pgroup": me, "tile": other}, device_id_type=MESH)

    def extent(h):
        return max(0, h * ROWS - 8), 128 if h == PARTS - 1 else (h + 1) * ROWS - 8

    def load(p, b, h, q):
        low, high = extent(h)
        rows = pl.ds(128 * b + low, high - low)
        source = (images, beams)[q]
        return pltpu.make_async_copy(source.at[p, rows, :], inp.at[p, q, rows, :], in_sem.at[p, b, h])

    def load_wait(p, b, h):
        low, high = extent(h)
        both = inp.at[p, :, pl.ds(128 * b + low, high - low), :]
        pltpu.make_async_copy(both, both, in_sem.at[p, b, h]).wait()

    def load_all(h, b):
        for p in range(2):
            for q in range(2):
                load(p, b, h, q).start()

    top = PARTS - 1
    load_all(top, 0)

    def to(src, dst, ssem, rsem, pgroup, z=None):
        return pltpu.make_async_remote_copy(
            src_ref=src, dst_ref=dst, send_sem=ssem, recv_sem=rsem,
            device_id={"pgroup": pgroup, "tile": tile if z is None else z}, device_id_type=MESH,
        )

    edge = jnp.zeros((STRIPS, 8, 128), jnp.float32)
    for p in range(2):
        for b in range(2):
            for q in range(2):
                cols[p, b, q, :, pl.ds(0, 8), :] = edge
                cols[p, b, q, :, pl.ds(136, 8), :] = edge
    for p in range(4):
        for h in range(PARTS):
            ra[h][p, STRIPS] = jnp.zeros((ROWS, 128), jnp.float32)
            rb[h][p, STRIPS] = jnp.zeros((ROWS, 128), jnp.float32)
        rc[p, STRIPS] = jnp.zeros((8, 128), jnp.float32)

    @pl.when(tile == 0)
    def _():
        hin[...] = jnp.zeros(hin.shape, jnp.float32)

    params = [
        to(row_block, their_row, par_send.at[0], par_recv.at[0], partner),
        to(col_block, their_col, par_send.at[1], par_recv.at[1], partner),
    ]
    first = lax.broadcasted_iota(jnp.int32, (8, 128), 1) == 0

    def band_columns(p, b, h):
        g = col_frac[p]
        load_wait(p, b, h)
        low, high = extent(h)
        for r in range(low, high, 8):
            rows = pl.ds(128 * b + r, 8)
            before = [jnp.zeros((8, 128), jnp.float32)] * 2
            for k in range(STRIPS):
                lanes = pl.ds(128 * k, 128)
                beam = inp[p, 1, rows, lanes]
                for q in range(2):
                    value = beam * inp[p, core if q == 0 else 1 - core, rows, lanes]
                    rolled = pltpu.roll(value, 1, 1)
                    moved = jnp.where(first, before[q], rolled)
                    before[q] = rolled
                    cols[p, b, q, k, pl.ds(r + 8, 8), :] = (1.0 - g) * value + g * moved

    def mix(p, b, q, k, start, length):
        f = row_frac[p]
        s = band[p, b]
        near = cols[p, b, q, k, pl.ds(start + 8 - s, length), :]
        far = cols[p, b, q, k, pl.ds(start + 7 - s, length), :]
        return (1.0 - f) * near + f * far

    def band_rows_a(p, h):
        def step(k, carry):
            ta[p, h, k] = mix(p, 0, 1, k, h * ROWS, ROWS)
            ra[h][p, k] = mix(p, 0, 0, k, h * ROWS, ROWS)
            return carry

        lax.fori_loop(0, STRIPS, step, 0)

    def band_rows_b(p, h):
        def step(k, carry):
            for q in (1, 0):
                part = mix(p, 1, q, k, h * ROWS, ROWS)
                spot = tb.at[p, h, k] if q else rb[h].at[p, k]
                if h == 0:
                    spot[pl.ds(0, 8), :] = part[0:8] + mix(p, 0, q, k, 128, 8)
                    spot[pl.ds(8, ROWS - 8), :] = part[8:ROWS]
                    low = tc if q else rc
                    low[p, k] = mix(p, 1, q, k, 128, 8)
                else:
                    spot[...] = part
            return carry

        lax.fori_loop(0, STRIPS, step, 0)

    def strips(p, n):
        kind, h = divmod(n, PARTS)
        mine = (ta.at[p, h], tb.at[p, h], tc.at[p])[kind]
        theirs = (ra[h], rb[h], rc)[kind]
        return to(mine, theirs.at[2 + p, pl.ds(0, STRIPS)], strip_send.at[n], strip_recv.at[n], partner)

    def strips_both(n):
        kind, h = divmod(n, PARTS)
        mine = (ta.at[:, h], tb.at[:, h], tc)[kind]
        theirs = (ra[h], rb[h], rc)[kind]
        return to(mine, theirs.at[pl.ds(2, 2), pl.ds(0, STRIPS)], strip_send.at[n], strip_recv.at[n], partner)

    for p in range(2):
        band_columns(p, 0, top)
        if p == 0:
            load_all(top, 1)
            for h in reversed(range(top)):
                load_all(h, 0)
                load_all(h, 1)
        band_rows_a(p, top)

    pl.semaphore_wait(barrier, 11)
    for copy in params:
        copy.start()
    for p in range(2):
        strips(p, top).start()
    for p in range(2):
        band_columns(p, 1, top)
        band_rows_b(p, top)
        strips(p, PARTS + top).start()

    for copy in params:
        copy.wait()
    offs = [row_block[p] - 4 * tile for p in range(2)] + [their_row[p] - 4 * tile for p in range(2)]
    shifts = [col_block[p] for p in range(2)] + [their_col[p] for p in range(2)]

    def column_of(rel, c):
        return lax.rem(u + rel, 4) * su + lax.rem(v + lax.div(c, 2), 4) * sv + lax.rem(c, 2)

    def block_of(k):
        return lax.rem(k + lax.div(k, CHUNKS - 4), 4)

    def generate(k, block, rel, h, early=False):
        def step(c, carry):
            j = column_of(rel, c)
            total = None
            extra = None
            for p in range(4):
                k_in = j - shifts[p]
                inside = (k_in >= 0) & (k_in < STRIPS)
                ia = jnp.where(inside & (block == offs[p]), k_in, STRIPS)
                part = ra[h][p, ia]
                total = part if total is None else total + part
                if not early:
                    ib = jnp.where(inside & (block == offs[p] + 1), k_in, STRIPS)
                    total = total + rb[h][p, ib]
                if h == 0:
                    ic = jnp.where(inside & (block == offs[p] + 2), k_in, STRIPS)
                    tail = rc[p, ic]
                    extra = tail if extra is None else extra + tail
            if h == 0:
                canvas[rel, k, c, pl.ds(0, 8), :] = total[0:8] + extra
                canvas[rel, k, c, pl.ds(8, ROWS - 8), :] = total[8:ROWS]
            else:
                canvas[rel, k, c] = total
            return carry

        lax.fori_loop(0, 8, step, 0)

        if h == 0:
            @pl.when(k == CHUNKS - 1)
            def _():
                canvas[rel, k, :, pl.ds(0, 8), :] = canvas[rel, k, :, pl.ds(0, 8), :] + hin[rel]

    def chunk(k):
        for h in range(PARTS):
            @pl.when(lax.div(k, 4) == PARTS - 1 - h)
            def _():
                block = block_of(k)
                generate(k, block, 2, h)
                send_a(k)
                for rel in (1, 3, 0):
                    generate(k, block, rel, h)

    def slot(k):
        return lax.rem(k, SLOTS)

    def copy_a(k, d):
        return to(canvas.at[2, k, pl.ds(4 * d, 4)], got_a.at[k, d], send_sem.at[0, slot(k)], recv_sem.at[0, slot(k)], (up, um)[d])

    def copy_b(k, d):
        return to(canvas.at[1 + 2 * d, k], got_b.at[k, d], send_sem.at[1, slot(k)], recv_sem.at[1, slot(k)], (up, um)[d])

    def copy_c(k, d):
        return to(canvas.at[0, k, 4 + d], got_c.at[k, d], send_sem.at[2, slot(k)], recv_sem.at[2, slot(k)], (vp, vm)[d])

    def copy_d(k, d, half):
        other = (vp, vm)[d] - core + half
        return to(canvas.at[0, k, 2 + 4 * d + half], got_d.at[k, 2 * core + d], send_sem.at[3, slot(k)], last_recv.at[k], other)

    def copy_e(k):
        return to(canvas.at[0, k, 1 - core], got_d.at[k, 4], send_sem.at[2, slot(k)], last_recv.at[k], partner)

    def await_recv(stage, k):
        if stage == 3:
            to(got_d.at[k], got_d.at[k], send_sem.at[3, 0], last_recv.at[k], partner).wait_recv()
        else:
            got = (got_a, got_b, got_c)[stage].at[k]
            to(got, got, send_sem.at[stage, 0], recv_sem.at[stage, slot(k)], partner).wait_recv()

    def await_send(stage, k):
        sent = (got_a.at[k], got_b.at[k], got_d.at[k, pl.ds(0, 3)], got_d.at[k, pl.ds(0, 4)])[stage]
        to(sent, sent, send_sem.at[stage, slot(k)], last_recv.at[0], partner).wait_send()

    def free(stage, k):
        @pl.when(k >= SLOTS)
        def _():
            await_send(stage, k - SLOTS)

    def send_a(k):
        copy_a(k, 0).start()
        copy_a(k, 1).start()

    def stage_b(k):
        await_recv(0, k)
        free(1, k)
        for d in range(2):
            part = pl.ds(4 * d, 4)
            canvas[1 + 2 * d, k, part] = canvas[1 + 2 * d, k, part] + got_a[k, d]
            copy_b(k, d).start()

    def stage_c(k):
        await_recv(1, k)
        free(2, k)
        for first_part, size in ((4, 2), (0, 4), (6, 2)):
            part = pl.ds(first_part, size)
            canvas[0, k, part] = canvas[0, k, part] + (got_b[k, 0, part] + got_b[k, 1, part])
            if first_part == 4:
                copy_c(k, 0).start()
                copy_c(k, 1).start()
        copy_e(k).start()

    def stage_d(k):
        await_recv(2, k)
        free(3, k)
        for d in range(2):
            spot = 2 + 5 * d
            canvas[0, k, spot] = canvas[0, k, spot] + got_c[k, d]
            copy_d(k, d, 0).start()
            copy_d(k, d, 1).start()

    def stage_f(k):
        await_recv(3, k)
        first_row = 128 * block_of(k) + ROWS * (PARTS - 1 - lax.div(k, 4))
        rows = pl.ds(pl.multiple_of(first_row, ROWS), ROWS)
        own = canvas[0, k, core] + (got_d[k, 2 * core] + got_d[k, 2 * core + 1])
        got = got_d[k, 4] + (got_d[k, 2 - 2 * core] + got_d[k, 3 - 2 * core])
        above = jnp.where(core == 0, own, got)
        below = jnp.where(core == 0, got, own)
        numer[rows, :] = above
        weight[rows, :] = below
        normalised[rows, :] = above / jnp.maximum(below, 0.05)

    strips_both(top).wait_recv()
    zero = jnp.int32(0)
    generate(zero, zero, 2, top, True)
    send_a(zero)
    for rel in (1, 3, 0):
        generate(zero, zero, rel, top, True)
    strips_both(PARTS + top).wait_recv()
    chunk_one = jnp.int32(1)
    generate(chunk_one, chunk_one, 2, top)
    send_a(chunk_one)
    for rel in (1, 3, 0):
        generate(chunk_one, chunk_one, rel, top)

    halo = to(hal, hin, hal_send, hal_recv, me, zp)

    def rest(h):
        for p in range(2):
            band_columns(p, 0, h)
            band_rows_a(p, h)
            strips(p, h).start()
            band_columns(p, 1, h)
            band_rows_b(p, h)
            strips(p, PARTS + h).start()
            if h == 0:
                strips(p, 2 * PARTS).start()

    def rest_wait(h):
        strips_both(h).wait_recv()
        strips_both(PARTS + h).wait_recv()
        if h == 0:
            strips_both(2 * PARTS).wait_recv()

    def send_halo():
        def step(n, carry):
            j = column_of(lax.div(n, 8), lax.rem(n, 8))
            total = None
            for p in range(4):
                k_in = j - shifts[p]
                ic = jnp.where((k_in >= 0) & (k_in < STRIPS) & (offs[p] == 2), k_in, STRIPS)
                tail = rc[p, ic]
                total = tail if total is None else total + tail
            hal[lax.div(n, 8), lax.rem(n, 8)] = total
            return carry

        lax.fori_loop(0, 32, step, 0)
        halo.start()

    def iteration(i, carry):
        for h in reversed(range(PARTS - 1)):
            k_first = 4 * (PARTS - 1 - h)

            @pl.when(i == k_first - 2)
            def _():
                rest(h)

            @pl.when(i == k_first)
            def _():
                rest_wait(h)
                if h == 0:
                    @pl.when(tile < 7)
                    def _():
                        send_halo()

        @pl.when((i == CHUNKS - 1) & (tile > 0))
        def _():
            halo.wait_recv()

        @pl.when(i < CHUNKS)
        def _():
            free(0, i)
            chunk(i)

        for lag, stage in ((LAG_B, stage_b), (LAG_D, stage_d), (LAG_F, stage_f), (LAG_C, stage_c)):
            @pl.when((i >= lag) & (i < CHUNKS + lag))
            def _():
                stage(i - lag)

        return carry

    if LAG_B == 1:
        stage_b(zero)
    lax.fori_loop(2, CHUNKS + LAG_F, iteration, 0)

    for stage in range(4):
        for k in range(CHUNKS - SLOTS, CHUNKS):
            await_send(stage, k)
    for n in range(2 * PARTS + 1):
        strips_both(n).wait_send()

    @pl.when(tile < 7)
    def _():
        halo.wait_send()


def store(numer, weight, normalised, numer_out, weight_out, normalised_out, sem):
    pairs = ((numer, numer_out), (weight, weight_out), (normalised, normalised_out))
    copies = [pltpu.make_async_copy(a, b, sem.at[n]) for n, (a, b) in enumerate(pairs)]
    for copy in copies:
        copy.start()
    for copy in copies:
        copy.wait()


def body(images, beams, row_block, col_block, band, row_frac, col_frac):
    f32 = jnp.float32
    vmem = lambda *shape: pltpu.VMEM(shape, f32)
    dma = pltpu.SemaphoreType.DMA
    piece = jax.ShapeDtypeStruct((SKY, 128), f32)
    hbm = pl.BlockSpec(memory_space=pl.ANY)
    smem = pl.BlockSpec(memory_space=pltpu.SMEM)
    local = pl.BlockSpec(memory_space=pltpu.VMEM)
    found = pl.pallas_call(
        kernel,
        out_shape=(pltpu.VMEM((SKY, 128), f32),) * 3,
        in_specs=[hbm, hbm, smem, smem, smem, smem, smem],
        out_specs=(local, local, local),
        scratch_shapes=[
            vmem(2, 2, 256, 2048),
            vmem(2, 2, 2, STRIPS, 144, 128),
            [vmem(4, STRIPS + 1, ROWS, 128) for _ in range(PARTS)],
            [vmem(4, STRIPS + 1, ROWS, 128) for _ in range(PARTS)],
            vmem(4, STRIPS + 1, 8, 128),
            vmem(2, PARTS, STRIPS, ROWS, 128),
            vmem(2, PARTS, STRIPS, ROWS, 128),
            vmem(2, STRIPS, 8, 128),
            vmem(4, CHUNKS, 8, ROWS, 128),
            vmem(4, 8, 8, 128),
            vmem(4, 8, 8, 128),
            vmem(CHUNKS, 2, 4, ROWS, 128),
            vmem(CHUNKS, 2, 8, ROWS, 128),
            vmem(CHUNKS, 2, ROWS, 128),
            vmem(CHUNKS, 5, ROWS, 128),
            pltpu.SMEM((2,), jnp.int32),
            pltpu.SMEM((2,), jnp.int32),
            dma((2, 2, PARTS)),
            dma((2,)),
            dma((2,)),
            dma((2 * PARTS + 1,)),
            dma((2 * PARTS + 1,)),
            dma,
            dma,
            dma((4, SLOTS)),
            dma((3, SLOTS)),
            dma((CHUNKS,)),
        ],
        compiler_params=pltpu.CompilerParams(
            collective_id=0, has_side_effects=True, vmem_limit_bytes=60_000_000
        ),
    )(images, beams, row_block, col_block, band, row_frac, col_frac)
    return pl.pallas_call(
        store,
        out_shape=(piece, piece, piece),
        in_specs=[local, local, local],
        out_specs=(hbm, hbm, hbm),
        scratch_shapes=[dma((3,))],
    )(*[pltpu.with_memory_space_constraint(a, pltpu.VMEM) for a in found])


def solution(mesh):
    return jax.shard_map(
        body,
        mesh=mesh,
        in_specs=(
            P(("pgroup", "tile"), None, None),
            P(("pgroup", "tile"), None, None),
            P(("pgroup", "tile")),
            P(("pgroup", "tile")),
            P(("pgroup", "tile"), None),
            P(("pgroup", "tile")),
            P(("pgroup", "tile")),
        ),
        out_specs=(P("tile", "pgroup"), P("tile", "pgroup"), P("tile", "pgroup")),
        check_vma=False,
    )
```

time: 79.6 us -> 66.6 us (0.84)
  Pallas kernels: 73.7 us -> 65.8 us
  local copies, waits for them, and re-layouts: 5.01 us -> 0 us
    pallas_call x1 -> x2, Pallas kernels: 73.7 us -> 65.8 us  [the longest x1 64.9 us: body(): pl.pallas_call(kernel, out_shape=(pltpu.VMEM((SKY, 128), f32),) * 3, in_s...]
    unnamed x3 -> x0, local copies, waits for them, and re-layouts: 5.01 us -> none
where the time goes in v2:
time: 66.6 us; the launch traced here: 66.5 us
  Pallas kernels  65.8 us (99%)
    pallas_call x1, Pallas kernels, body(): pl.pallas_call(kernel, out_shape=(pltpu.VMEM((SKY, 128), f32),) * 3, in_s...  64.9 us

profile of v2, /device:TPU:1, one launch (start us, length us, event | category | flops | bytes accessed | tf_op | source)
XLA Modules:
  0.0 66.5 jit_solution(13102160582078943655)
XLA Ops:
  0.6 64.9 %shard_map.94 = (f32[512,128]{1,0:T(8,128)S(1)}, f32[512,128]{1,0:T(8,128)S(1)}, f32[512,128]{1,0:T(8,128)S(1)}) custom-call(f32[2,256,2048]{2,1,0:T(8,128)} %images.1, f32[2,256,2048]{2,1,0:T(8,128)} %beams.1, s32[2]{0:T(128)} %row_block.1, s32[2]{0:T(128)} %col_block.1, s32[2,2]{1,0:T(2,128)} %band.1, f32[2]{0:T(128)} %row_frac.1, f32[2]{0:T(128)} %col_frac.1), custom_call_target="tpu_custom_call" | custom-call | tf_op jit(solution)/shard_map/pallas_call | solution.py:421
  65.5 0.9 %shard_map.95 = (f32[512,128]{1,0:T(8,128)}, f32[512,128]{1,0:T(8,128)}, f32[512,128]{1,0:T(8,128)}) custom-call(f32[512,128]{1,0:T(8,128)S(1)} %get-tuple-element.6.numer, f32[512,128]{1,0:T(8,128)S(1)} %get-tuple-element.7.weight, f32[512,128]{1,0:T(8,128)S(1)} %get-tuple-element.8.normalised), custom_call_target="tpu_custom_call" | custom-call | tf_op jit(solution)/shard_map/pallas_call | solution.py:459

commit v3 on v2

--- a/solution.py
+++ b/solution.py
@@ -7,21 +7,22 @@
 
 MESH = pl.DeviceIdType.MESH
 STRIPS = 16
-ROWS = 64
+ROWS = 32
 PARTS = 128 // ROWS
 CHUNKS = 4 * PARTS
+LAST = CHUNKS - 1
 SKY = 512
-SLOTS = 4
-LAG_B, LAG_C, LAG_D, LAG_F = 1, 2, 3, 4
+SEND_SLOTS, RECV_SLOTS = 4, 8
+LAG_B, LAG_C, LAG_D, LAG_F = 3, 6, 9, 12
 
 
 def kernel(
-    images, beams, row_block, col_block, band, row_frac, col_frac,
+    images, beams, row_block_in, col_block_in, band_in, row_frac_in, col_frac_in,
     numer, weight, normalised,
     inp, cols, ra, rb, rc, ta, tb, tc, canvas, hal, hin,
-    got_a, got_b, got_c, got_d, their_row, their_col,
-    in_sem, par_send, par_recv, strip_send, strip_recv, hal_send, hal_recv,
-    send_sem, recv_sem, last_recv,
+    got_a, got_b, got_c, got_d, row_block, col_block, band, row_frac, col_frac, their_row, their_col,
+    in_sem, scalar_sem, par_send, par_recv, strip_send, strip_recv, hal_send, hal_recv,
+    send_sem, recv_sem, last_recv, end_send,
 ):
     me = lax.axis_index("pgroup")
     tile = lax.axis_index("tile")
@@ -36,15 +37,8 @@
     um = lax.rem(u + 3, 4) * su + v * sv + core
     vp = u * su + lax.rem(v + 1, 4) * sv + core
     vm = u * su + lax.rem(v + 3, 4) * sv + core
-    zp, zm = lax.rem(tile + 1, 8), lax.rem(tile + 7, 8)
-
-    barrier = pltpu.get_barrier_semaphore()
-    for chip in (up - core, um - core, vp - core, vm - core):
-        for other in (chip, chip + 1):
-            pl.semaphore_signal(barrier, inc=1, device_id={"pgroup": other, "tile": tile}, device_id_type=MESH)
-    pl.semaphore_signal(barrier, inc=1, device_id={"pgroup": partner, "tile": tile}, device_id_type=MESH)
-    for other in (zp, zm):
-        pl.semaphore_signal(barrier, inc=1, device_id={"pgroup": me, "tile": other}, device_id_type=MESH)
+    uq = lax.rem(u + 2, 4) * su + v * sv + core
+    vq = u * su + lax.rem(v + 2, 4) * sv + core
 
     def extent(h):
         return max(0, h * ROWS - 8), 128 if h == PARTS - 1 else (h + 1) * ROWS - 8
@@ -65,8 +59,27 @@
             for q in range(2):
                 load(p, b, h, q).start()
 
+    scalars = [
+        pltpu.make_async_copy(src, dst, scalar_sem.at[n])
+        for n, (src, dst) in enumerate((
+            (col_frac_in, col_frac), (row_frac_in, row_frac), (band_in, band), (row_block_in, row_block), (col_block_in, col_block),
+        ))
+    ]
+
     top = PARTS - 1
     load_all(top, 0)
+    for copy in scalars:
+        copy.start()
+
+    barrier = pltpu.get_barrier_semaphore()
+    for chip in (up - core, um - core, vp - core, vm - core, uq - core, vq - core):
+        for other in (chip, chip + 1):
+            pl.semaphore_signal(barrier, inc=1, device_id={"pgroup": other, "tile": tile}, device_id_type=MESH)
+    pl.semaphore_signal(barrier, inc=1, device_id={"pgroup": partner, "tile": tile}, device_id_type=MESH)
+    for has, other in ((tile < 7, tile + 1), (tile > 0, tile - 1)):
+        @pl.when(has)
+        def _():
+            pl.semaphore_signal(barrier, inc=1, device_id={"pgroup": me, "tile": other}, device_id_type=MESH)
 
     def to(src, dst, ssem, rsem, pgroup, z=None):
         return pltpu.make_async_remote_copy(
@@ -156,6 +169,8 @@
         theirs = (ra[h], rb[h], rc)[kind]
         return to(mine, theirs.at[pl.ds(2, 2), pl.ds(0, STRIPS)], strip_send.at[n], strip_recv.at[n], partner)
 
+    for copy in scalars:
+        copy.wait()
     for p in range(2):
         band_columns(p, 0, top)
         if p == 0:
@@ -165,7 +180,7 @@
                 load_all(h, 1)
         band_rows_a(p, top)
 
-    pl.semaphore_wait(barrier, 11)
+    pl.semaphore_wait(barrier, 13 + jnp.where(tile < 7, 1, 0) + jnp.where(tile > 0, 1, 0))
     for copy in params:
         copy.start()
     for p in range(2):
@@ -214,60 +229,64 @@
         lax.fori_loop(0, 8, step, 0)
 
         if h == 0:
-            @pl.when(k == CHUNKS - 1)
+            @pl.when(k == LAST)
             def _():
                 canvas[rel, k, :, pl.ds(0, 8), :] = canvas[rel, k, :, pl.ds(0, 8), :] + hin[rel]
 
-    def chunk(k):
+    def canvas_parts(k, rels):
         for h in range(PARTS):
             @pl.when(lax.div(k, 4) == PARTS - 1 - h)
             def _():
-                block = block_of(k)
-                generate(k, block, 2, h)
-                send_a(k)
-                for rel in (1, 3, 0):
-                    generate(k, block, rel, h)
+                for rel in rels:
+                    generate(k, block_of(k), rel, h)
+
+    def send_slot(k):
+        return lax.rem(k, SEND_SLOTS)
 
     def slot(k):
-        return lax.rem(k, SLOTS)
+        return lax.rem(k, RECV_SLOTS)
 
     def copy_a(k, d):
-        return to(canvas.at[2, k, pl.ds(4 * d, 4)], got_a.at[k, d], send_sem.at[0, slot(k)], recv_sem.at[0, slot(k)], (up, um)[d])
+        return to(canvas.at[2, k, pl.ds(4 * d, 4)], got_a.at[k, d], send_sem.at[0, send_slot(k)], recv_sem.at[0, slot(k)], (up, um)[d])
 
     def copy_b(k, d):
-        return to(canvas.at[1 + 2 * d, k], got_b.at[k, d], send_sem.at[1, slot(k)], recv_sem.at[1, slot(k)], (up, um)[d])
+        return to(canvas.at[1 + 2 * d, k], got_b.at[k, d], send_sem.at[1, send_slot(k)], recv_sem.at[1, slot(k)], (up, um)[d])
 
     def copy_c(k, d):
-        return to(canvas.at[0, k, 4 + d], got_c.at[k, d], send_sem.at[2, slot(k)], recv_sem.at[2, slot(k)], (vp, vm)[d])
+        return to(canvas.at[0, k, 4 + d], got_c.at[k, d], send_sem.at[2, send_slot(k)], recv_sem.at[2, slot(k)], (vp, vm)[d])
 
     def copy_d(k, d, half):
         other = (vp, vm)[d] - core + half
-        return to(canvas.at[0, k, 2 + 4 * d + half], got_d.at[k, 2 * core + d], send_sem.at[3, slot(k)], last_recv.at[k], other)
+        return to(canvas.at[0, k, 2 + 4 * d + half], got_d.at[k, 2 * core + d], send_sem.at[3, send_slot(k)], last_recv.at[k], other)
 
     def copy_e(k):
-        return to(canvas.at[0, k, 1 - core], got_d.at[k, 4], send_sem.at[2, slot(k)], last_recv.at[k], partner)
+        return to(canvas.at[0, k, 1 - core], got_d.at[k, 4], send_sem.at[2, send_slot(k)], last_recv.at[k], partner)
 
     def await_recv(stage, k):
-        if stage == 3:
-            to(got_d.at[k], got_d.at[k], send_sem.at[3, 0], last_recv.at[k], partner).wait_recv()
+        if stage >= 3:
+            got = got_d.at[k, pl.ds(0, 5 if stage == 3 else 7)]
+            to(got, got, send_sem.at[3, 0], last_recv.at[k], partner).wait_recv()
         else:
             got = (got_a, got_b, got_c)[stage].at[k]
             to(got, got, send_sem.at[stage, 0], recv_sem.at[stage, slot(k)], partner).wait_recv()
 
     def await_send(stage, k):
         sent = (got_a.at[k], got_b.at[k], got_d.at[k, pl.ds(0, 3)], got_d.at[k, pl.ds(0, 4)])[stage]
-        to(sent, sent, send_sem.at[stage, slot(k)], last_recv.at[0], partner).wait_send()
+        to(sent, sent, send_sem.at[stage, send_slot(k)], last_recv.at[0], partner).wait_send()
 
     def free(stage, k):
-        @pl.when(k >= SLOTS)
+        @pl.when(k >= SEND_SLOTS)
         def _():
-            await_send(stage, k - SLOTS)
-
-    def send_a(k):
+            await_send(stage, k - SEND_SLOTS)
+
+    def stage_a(k):
+        free(0, k)
+        canvas_parts(k, (2,))
         copy_a(k, 0).start()
         copy_a(k, 1).start()
 
     def stage_b(k):
+        canvas_parts(k, (1, 3, 0))
         await_recv(0, k)
         free(1, k)
         for d in range(2):
@@ -295,43 +314,51 @@
             copy_d(k, d, 0).start()
             copy_d(k, d, 1).start()
 
-    def stage_f(k):
-        await_recv(3, k)
+    def copy_end(n, half):
+        other = (vp, vm, vq)[n] - core + half
+        piece = canvas.at[0, LAST, (2, 6, 4)[n] + half]
+        return to(piece, got_d.at[LAST, (2 * core, 2 * core + 1, 5 + core)[n]], end_send, last_recv.at[LAST], other)
+
+    def copy_end_own():
+        return to(canvas.at[0, LAST, 1 - core], got_d.at[LAST, 4], end_send, last_recv.at[LAST], partner)
+
+    def stage_end():
+        await_recv(1, LAST)
+        for n, first_part in ((2, 4), (0, 2), (1, 6)):
+            part = pl.ds(first_part, 2)
+            canvas[0, LAST, part] = canvas[0, LAST, part] + (got_b[LAST, 0, part] + got_b[LAST, 1, part])
+            for half in range(2):
+                copy_end(n, half).start()
+        part = pl.ds(0, 2)
+        canvas[0, LAST, part] = canvas[0, LAST, part] + (got_b[LAST, 0, part] + got_b[LAST, 1, part])
+        copy_end_own().start()
+
+    def stage_f(k, last=False):
+        await_recv(4 if last else 3, k)
         first_row = 128 * block_of(k) + ROWS * (PARTS - 1 - lax.div(k, 4))
         rows = pl.ds(pl.multiple_of(first_row, ROWS), ROWS)
         own = canvas[0, k, core] + (got_d[k, 2 * core] + got_d[k, 2 * core + 1])
         got = got_d[k, 4] + (got_d[k, 2 - 2 * core] + got_d[k, 3 - 2 * core])
+        if last:
+            own = own + got_d[k, 5 + core]
+            got = got + got_d[k, 6 - core]
         above = jnp.where(core == 0, own, got)
         below = jnp.where(core == 0, got, own)
         numer[rows, :] = above
         weight[rows, :] = below
         normalised[rows, :] = above / jnp.maximum(below, 0.05)
 
-    strips_both(top).wait_recv()
-    zero = jnp.int32(0)
-    generate(zero, zero, 2, top, True)
-    send_a(zero)
-    for rel in (1, 3, 0):
-        generate(zero, zero, rel, top, True)
-    strips_both(PARTS + top).wait_recv()
-    chunk_one = jnp.int32(1)
-    generate(chunk_one, chunk_one, 2, top)
-    send_a(chunk_one)
-    for rel in (1, 3, 0):
-        generate(chunk_one, chunk_one, rel, top)
-
-    halo = to(hal, hin, hal_send, hal_recv, me, zp)
-
-    def rest(h):
-        for p in range(2):
-            band_columns(p, 0, h)
-            band_rows_a(p, h)
-            strips(p, h).start()
-            band_columns(p, 1, h)
-            band_rows_b(p, h)
-            strips(p, PARTS + h).start()
-            if h == 0:
-                strips(p, 2 * PARTS).start()
+    halo = to(hal, hin, hal_send, hal_recv, me, lax.rem(tile + 1, 8))
+
+    def rest(h, p):
+        band_columns(p, 0, h)
+        band_rows_a(p, h)
+        strips(p, h).start()
+        band_columns(p, 1, h)
+        band_rows_b(p, h)
+        strips(p, PARTS + h).start()
+        if h == 0:
+            strips(p, 2 * PARTS).start()
 
     def rest_wait(h):
         strips_both(h).wait_recv()
@@ -356,13 +383,7 @@
 
     def iteration(i, carry):
         for h in reversed(range(PARTS - 1)):
-            k_first = 4 * (PARTS - 1 - h)
-
-            @pl.when(i == k_first - 2)
-            def _():
-                rest(h)
-
-            @pl.when(i == k_first)
+            @pl.when(i == part_start(h))
             def _():
                 rest_wait(h)
                 if h == 0:
@@ -370,29 +391,56 @@
                     def _():
                         send_halo()
 
-        @pl.when((i == CHUNKS - 1) & (tile > 0))
+        @pl.when((i == LAST) & (tile > 0))
         def _():
             halo.wait_recv()
 
         @pl.when(i < CHUNKS)
         def _():
-            free(0, i)
-            chunk(i)
-
-        for lag, stage in ((LAG_B, stage_b), (LAG_D, stage_d), (LAG_F, stage_f), (LAG_C, stage_c)):
-            @pl.when((i >= lag) & (i < CHUNKS + lag))
+            stage_a(i)
+
+        for h in reversed(range(PARTS - 1)):
+            for p in range(2):
+                if part_start(h) - 2 + p >= LAG_B:
+                    @pl.when(i == part_start(h) - 2 + p)
+                    def _():
+                        rest(h, p)
+
+        stages = ((LAG_B, stage_b, CHUNKS), (LAG_D, stage_d, LAST), (LAG_F, stage_f, LAST), (LAG_C, stage_c, LAST))
+        for lag, stage, count in stages:
+            @pl.when((i >= lag) & (i < count + lag))
             def _():
                 stage(i - lag)
 
+        @pl.when(i == LAST + LAG_C)
+        def _():
+            stage_end()
+
         return carry
 
-    if LAG_B == 1:
-        stage_b(zero)
-    lax.fori_loop(2, CHUNKS + LAG_F, iteration, 0)
+    def part_start(h):
+        return 4 * (PARTS - 1 - h)
+
+    strips_both(top).wait_recv()
+    generate(0, 0, 2, top, True)
+    copy_a(0, 0).start()
+    copy_a(0, 1).start()
+    strips_both(PARTS + top).wait_recv()
+    for i in range(1, LAG_B):
+        generate(i, i, 2, top)
+        copy_a(i, 0).start()
+        copy_a(i, 1).start()
+        for p in range(2):
+            if i == part_start(top - 1) - 2 + p:
+                rest(top - 1, p)
+    lax.fori_loop(LAG_B, LAST + LAG_F, iteration, 0)
+    stage_f(LAST, True)
 
     for stage in range(4):
-        for k in range(CHUNKS - SLOTS, CHUNKS):
+        count = CHUNKS if stage < 2 else LAST
+        for k in range(count - SEND_SLOTS, count):
             await_send(stage, k)
+    to(got_d.at[LAST], got_d.at[LAST], end_send, last_recv.at[0], partner).wait_send()
     for n in range(2 * PARTS + 1):
         strips_both(n).wait_send()
 
@@ -416,12 +464,11 @@
     dma = pltpu.SemaphoreType.DMA
     piece = jax.ShapeDtypeStruct((SKY, 128), f32)
     hbm = pl.BlockSpec(memory_space=pl.ANY)
-    smem = pl.BlockSpec(memory_space=pltpu.SMEM)
     local = pl.BlockSpec(memory_space=pltpu.VMEM)
     found = pl.pallas_call(
         kernel,
         out_shape=(pltpu.VMEM((SKY, 128), f32),) * 3,
-        in_specs=[hbm, hbm, smem, smem, smem, smem, smem],
+        in_specs=[hbm] * 7,
         out_specs=(local, local, local),
         scratch_shapes=[
             vmem(2, 2, 256, 2048),
@@ -438,19 +485,26 @@
             vmem(CHUNKS, 2, 4, ROWS, 128),
             vmem(CHUNKS, 2, 8, ROWS, 128),
             vmem(CHUNKS, 2, ROWS, 128),
-            vmem(CHUNKS, 5, ROWS, 128),
+            vmem(CHUNKS, 7, ROWS, 128),
+            pltpu.SMEM((2,), jnp.int32),
+            pltpu.SMEM((2,), jnp.int32),
+            pltpu.SMEM((2, 2), jnp.int32),
+            pltpu.SMEM((2,), f32),
+            pltpu.SMEM((2,), f32),
             pltpu.SMEM((2,), jnp.int32),
             pltpu.SMEM((2,), jnp.int32),
             dma((2, 2, PARTS)),
+            dma((5,)),
             dma((2,)),
             dma((2,)),
             dma((2 * PARTS + 1,)),
             dma((2 * PARTS + 1,)),
             dma,
             dma,
-            dma((4, SLOTS)),
-            dma((3, SLOTS)),
+            dma((4, SEND_SLOTS)),
+            dma((3, RECV_SLOTS)),
             dma((CHUNKS,)),
+            dma,
         ],
         compiler_params=pltpu.CompilerParams(
             collective_id=0, has_side_effects=True, vmem_limit_bytes=60_000_000

time: 66.6 us -> 59.4 us (0.89)
  Pallas kernels: 65.8 us -> 58.7 us
    pallas_call x1, Pallas kernels: 64.9 us -> 57.8 us  [body(): pl.pallas_call(kernel, out_shape=(pltpu.VMEM((SKY, 128), f32),) * 3, in_s...]
where the time goes in v3:
time: 59.4 us; the launch traced here: 59.3 us
  Pallas kernels  58.7 us (99%)
  between operations  0.64 us (1%)
    pallas_call x1, Pallas kernels, body(): pl.pallas_call(kernel, out_shape=(pltpu.VMEM((SKY, 128), f32),) * 3, in_s...  57.8 us

profile of v3, /device:TPU:1, one launch (start us, length us, event | category | flops | bytes accessed | tf_op | source)
XLA Modules:
  0.0 59.3 jit_solution(2189259270231566521)
XLA Ops:
  0.6 57.8 %shard_map.94 = (f32[512,128]{1,0:T(8,128)S(1)}, f32[512,128]{1,0:T(8,128)S(1)}, f32[512,128]{1,0:T(8,128)S(1)}) custom-call(f32[2,256,2048]{2,1,0:T(8,128)} %images.1, f32[2,256,2048]{2,1,0:T(8,128)} %beams.1, s32[2]{0:T(128)} %row_block_in.1, s32[2]{0:T(128)} %col_block_in.1, s32[2,2]{1,0:T(2,128)} %band_in.1, f32[2]{0:T(128)} %row_frac_in.1, f32[2]{0:T(128)} %col_frac_in.1), custom_call_target="tpu_custom_call" | custom-call | tf_op jit(solution)/shard_map/pallas_call | solution.py:468
  58.4 0.9 %shard_map.95 = (f32[512,128]{1,0:T(8,128)}, f32[512,128]{1,0:T(8,128)}, f32[512,128]{1,0:T(8,128)}) custom-call(f32[512,128]{1,0:T(8,128)S(1)} %get-tuple-element.6.numer, f32[512,128]{1,0:T(8,128)S(1)} %get-tuple-element.7.weight, f32[512,128]{1,0:T(8,128)S(1)} %get-tuple-element.8.normalised), custom_call_target="tpu_custom_call" | custom-call | tf_op jit(solution)/shard_map/pallas_call | solution.py:513

commit v4 on v3

--- a/solution.py
+++ b/solution.py
@@ -11,8 +11,9 @@
 PARTS = 128 // ROWS
 CHUNKS = 4 * PARTS
 LAST = CHUNKS - 1
+UNROLL = 2
 SKY = 512
-SEND_SLOTS, RECV_SLOTS = 4, 8
+SEND_SLOTS, RECV_SLOTS = (4, 4, 4, 4), (8, 8, 8)
 LAG_B, LAG_C, LAG_D, LAG_F = 3, 6, 9, 12
 
 
@@ -37,22 +38,32 @@
     um = lax.rem(u + 3, 4) * su + v * sv + core
     vp = u * su + lax.rem(v + 1, 4) * sv + core
     vm = u * su + lax.rem(v + 3, 4) * sv + core
-    uq = lax.rem(u + 2, 4) * su + v * sv + core
     vq = u * su + lax.rem(v + 2, 4) * sv + core
 
     def extent(h):
         return max(0, h * ROWS - 8), 128 if h == PARTS - 1 else (h + 1) * ROWS - 8
+
+    top = PARTS - 1
 
     def load(p, b, h, q):
         low, high = extent(h)
         rows = pl.ds(128 * b + low, high - low)
         source = (images, beams)[q]
-        return pltpu.make_async_copy(source.at[p, rows, :], inp.at[p, q, rows, :], in_sem.at[p, b, h])
+        return pltpu.make_async_copy(source.at[p, rows, :], inp.at[p, q, rows, :], in_sem.at[input_sem(p, b, h)])
+
+    def input_sem(p, b, h):
+        return 2 * PARTS if p == 1 and b == 0 and h == top else 2 * h + b
 
     def load_wait(p, b, h):
         low, high = extent(h)
-        both = inp.at[p, :, pl.ds(128 * b + low, high - low), :]
-        pltpu.make_async_copy(both, both, in_sem.at[p, b, h]).wait()
+        rows = pl.ds(128 * b + low, high - low)
+        if b == 0 and h == top:
+            part = inp.at[p, :, rows, :]
+        elif p == 0:
+            part = inp.at[:, :, rows, :]
+        else:
+            return
+        pltpu.make_async_copy(part, part, in_sem.at[input_sem(p, b, h)]).wait()
 
     def load_all(h, b):
         for p in range(2):
@@ -66,13 +77,12 @@
         ))
     ]
 
-    top = PARTS - 1
     load_all(top, 0)
     for copy in scalars:
         copy.start()
 
     barrier = pltpu.get_barrier_semaphore()
-    for chip in (up - core, um - core, vp - core, vm - core, uq - core, vq - core):
+    for chip in (up - core, um - core, vp - core, vm - core):
         for other in (chip, chip + 1):
             pl.semaphore_signal(barrier, inc=1, device_id={"pgroup": other, "tile": tile}, device_id_type=MESH)
     pl.semaphore_signal(barrier, inc=1, device_id={"pgroup": partner, "tile": tile}, device_id_type=MESH)
@@ -180,7 +190,7 @@
                 load_all(h, 1)
         band_rows_a(p, top)
 
-    pl.semaphore_wait(barrier, 13 + jnp.where(tile < 7, 1, 0) + jnp.where(tile > 0, 1, 0))
+    pl.semaphore_wait(barrier, 9 + jnp.where(tile < 7, 1, 0) + jnp.where(tile > 0, 1, 0))
     for copy in params:
         copy.start()
     for p in range(2):
@@ -202,31 +212,36 @@
         return lax.rem(k + lax.div(k, CHUNKS - 4), 4)
 
     def generate(k, block, rel, h, early=False):
+        reach = [
+            [jnp.where(block == offs[p] + n, STRIPS, 0) for n in range(3)] for p in range(4)
+        ]
+
+        def pick(k_in, limit):
+            return jnp.where((k_in >= 0) & (k_in < limit), k_in, STRIPS)
+
         def step(c, carry):
-            j = column_of(rel, c)
-            total = None
-            extra = None
-            for p in range(4):
-                k_in = j - shifts[p]
-                inside = (k_in >= 0) & (k_in < STRIPS)
-                ia = jnp.where(inside & (block == offs[p]), k_in, STRIPS)
-                part = ra[h][p, ia]
-                total = part if total is None else total + part
-                if not early:
-                    ib = jnp.where(inside & (block == offs[p] + 1), k_in, STRIPS)
-                    total = total + rb[h][p, ib]
+            for half in range(UNROLL):
+                spot = UNROLL * c + half
+                j = column_of(rel, spot)
+                total = None
+                extra = None
+                for p in range(4):
+                    k_in = j - shifts[p]
+                    part = ra[h][p, pick(k_in, reach[p][0])]
+                    total = part if total is None else total + part
+                    if not early:
+                        total = total + rb[h][p, pick(k_in, reach[p][1])]
+                    if h == 0:
+                        tail = rc[p, pick(k_in, reach[p][2])]
+                        extra = tail if extra is None else extra + tail
                 if h == 0:
-                    ic = jnp.where(inside & (block == offs[p] + 2), k_in, STRIPS)
-                    tail = rc[p, ic]
-                    extra = tail if extra is None else extra + tail
-            if h == 0:
-                canvas[rel, k, c, pl.ds(0, 8), :] = total[0:8] + extra
-                canvas[rel, k, c, pl.ds(8, ROWS - 8), :] = total[8:ROWS]
-            else:
-                canvas[rel, k, c] = total
+                    canvas[rel, k, spot, pl.ds(0, 8), :] = total[0:8] + extra
+                    canvas[rel, k, spot, pl.ds(8, ROWS - 8), :] = total[8:ROWS]
+                else:
+                    canvas[rel, k, spot] = total
             return carry
 
-        lax.fori_loop(0, 8, step, 0)
+        lax.fori_loop(0, 8 // UNROLL, step, 0)
 
         if h == 0:
             @pl.when(k == LAST)
@@ -240,44 +255,44 @@
                 for rel in rels:
                     generate(k, block_of(k), rel, h)
 
-    def send_slot(k):
-        return lax.rem(k, SEND_SLOTS)
-
-    def slot(k):
-        return lax.rem(k, RECV_SLOTS)
+    def sent(stage, k):
+        return send_sem.at[sum(SEND_SLOTS[:stage]) + lax.rem(k, SEND_SLOTS[stage])]
+
+    def landed(stage, k):
+        return recv_sem.at[sum(RECV_SLOTS[:stage]) + lax.rem(k, RECV_SLOTS[stage])]
 
     def copy_a(k, d):
-        return to(canvas.at[2, k, pl.ds(4 * d, 4)], got_a.at[k, d], send_sem.at[0, send_slot(k)], recv_sem.at[0, slot(k)], (up, um)[d])
+        return to(canvas.at[2, k, pl.ds(4 * d, 4)], got_a.at[k, d], sent(0, k), landed(0, k), (up, um)[d])
 
     def copy_b(k, d):
-        return to(canvas.at[1 + 2 * d, k], got_b.at[k, d], send_sem.at[1, send_slot(k)], recv_sem.at[1, slot(k)], (up, um)[d])
+        return to(canvas.at[1 + 2 * d, k], got_b.at[k, d], sent(1, k), landed(1, k), (up, um)[d])
 
     def copy_c(k, d):
-        return to(canvas.at[0, k, 4 + d], got_c.at[k, d], send_sem.at[2, send_slot(k)], recv_sem.at[2, slot(k)], (vp, vm)[d])
+        return to(canvas.at[0, k, 4 + d], got_c.at[k, d], sent(2, k), landed(2, k), (vp, vm)[d])
 
     def copy_d(k, d, half):
         other = (vp, vm)[d] - core + half
-        return to(canvas.at[0, k, 2 + 4 * d + half], got_d.at[k, 2 * core + d], send_sem.at[3, send_slot(k)], last_recv.at[k], other)
+        return to(canvas.at[0, k, 2 + 4 * d + half], got_d.at[k, 2 * core + d], sent(3, k), last_recv.at[k], other)
 
     def copy_e(k):
-        return to(canvas.at[0, k, 1 - core], got_d.at[k, 4], send_sem.at[2, send_slot(k)], last_recv.at[k], partner)
+        return to(canvas.at[0, k, 1 - core], got_d.at[k, 4], sent(2, k), last_recv.at[k], partner)
 
     def await_recv(stage, k):
         if stage >= 3:
             got = got_d.at[k, pl.ds(0, 5 if stage == 3 else 7)]
-            to(got, got, send_sem.at[3, 0], last_recv.at[k], partner).wait_recv()
+            to(got, got, end_send, last_recv.at[k], partner).wait_recv()
         else:
             got = (got_a, got_b, got_c)[stage].at[k]
-            to(got, got, send_sem.at[stage, 0], recv_sem.at[stage, slot(k)], partner).wait_recv()
+            to(got, got, end_send, landed(stage, k), partner).wait_recv()
 
     def await_send(stage, k):
-        sent = (got_a.at[k], got_b.at[k], got_d.at[k, pl.ds(0, 3)], got_d.at[k, pl.ds(0, 4)])[stage]
-        to(sent, sent, send_sem.at[stage, send_slot(k)], last_recv.at[0], partner).wait_send()
+        size = (got_a.at[k], got_b.at[k], got_d.at[k, pl.ds(0, 3)], got_d.at[k, pl.ds(0, 4)])[stage]
+        to(size, size, sent(stage, k), last_recv.at[0], partner).wait_send()
 
     def free(stage, k):
-        @pl.when(k >= SEND_SLOTS)
-        def _():
-            await_send(stage, k - SEND_SLOTS)
+        @pl.when(k >= SEND_SLOTS[stage])
+        def _():
+            await_send(stage, k - SEND_SLOTS[stage])
 
     def stage_a(k):
         free(0, k)
@@ -286,7 +301,10 @@
         copy_a(k, 1).start()
 
     def stage_b(k):
-        canvas_parts(k, (1, 3, 0))
+        @pl.when(k > 0)
+        def _():
+            canvas_parts(k, (1, 3, 0))
+
         await_recv(0, k)
         free(1, k)
         for d in range(2):
@@ -386,10 +404,6 @@
             @pl.when(i == part_start(h))
             def _():
                 rest_wait(h)
-                if h == 0:
-                    @pl.when(tile < 7)
-                    def _():
-                        send_halo()
 
         @pl.when((i == LAST) & (tile > 0))
         def _():
@@ -401,8 +415,8 @@
 
         for h in reversed(range(PARTS - 1)):
             for p in range(2):
-                if part_start(h) - 2 + p >= LAG_B:
-                    @pl.when(i == part_start(h) - 2 + p)
+                if rest_step(h, p) >= LAG_B:
+                    @pl.when(i == rest_step(h, p))
                     def _():
                         rest(h, p)
 
@@ -416,29 +430,38 @@
         def _():
             stage_end()
 
+        @pl.when((i == part_start(0)) & (tile < 7))
+        def _():
+            send_halo()
+
         return carry
 
     def part_start(h):
         return 4 * (PARTS - 1 - h)
+
+    def rest_step(h, p):
+        return part_start(h) - (2 if h == top - 1 else 3) + p
 
     strips_both(top).wait_recv()
     generate(0, 0, 2, top, True)
     copy_a(0, 0).start()
     copy_a(0, 1).start()
+    for rel in (1, 3, 0):
+        generate(0, 0, rel, top, True)
     strips_both(PARTS + top).wait_recv()
     for i in range(1, LAG_B):
         generate(i, i, 2, top)
         copy_a(i, 0).start()
         copy_a(i, 1).start()
         for p in range(2):
-            if i == part_start(top - 1) - 2 + p:
+            if i == rest_step(top - 1, p):
                 rest(top - 1, p)
     lax.fori_loop(LAG_B, LAST + LAG_F, iteration, 0)
     stage_f(LAST, True)
 
     for stage in range(4):
         count = CHUNKS if stage < 2 else LAST
-        for k in range(count - SEND_SLOTS, count):
+        for k in range(count - SEND_SLOTS[stage], count):
             await_send(stage, k)
     to(got_d.at[LAST], got_d.at[LAST], end_send, last_recv.at[0], partner).wait_send()
     for n in range(2 * PARTS + 1):
@@ -493,7 +516,7 @@
             pltpu.SMEM((2,), f32),
             pltpu.SMEM((2,), jnp.int32),
             pltpu.SMEM((2,), jnp.int32),
-            dma((2, 2, PARTS)),
+            dma((2 * PARTS + 1,)),
             dma((5,)),
             dma((2,)),
             dma((2,)),
@@ -501,8 +524,8 @@
             dma((2 * PARTS + 1,)),
             dma,
             dma,
-            dma((4, SEND_SLOTS)),
-            dma((3, RECV_SLOTS)),
+            dma((sum(SEND_SLOTS),)),
+            dma((sum(RECV_SLOTS),)),
             dma((CHUNKS,)),
             dma,
         ],

time: 59.4 us -> 59.1 us (level)
  no operation moved by 1% of the time
where the time goes in v4:
time: 59.1 us; the launch traced here: 58.9 us
  Pallas kernels  58.3 us (99%)
  between operations  0.64 us (1%)
    pallas_call x1, Pallas kernels, body(): pl.pallas_call(kernel, out_shape=(pltpu.VMEM((SKY, 128), f32),) * 3, in_s...  57.4 us

profile of v4, /device:TPU:1, one launch (start us, length us, event | category | flops | bytes accessed | tf_op | source)
XLA Modules:
  0.0 58.9 jit_solution(3500360107595812652)
XLA Ops:
  0.6 57.4 %shard_map.94 = (f32[512,128]{1,0:T(8,128)S(1)}, f32[512,128]{1,0:T(8,128)S(1)}, f32[512,128]{1,0:T(8,128)S(1)}) custom-call(f32[2,256,2048]{2,1,0:T(8,128)} %images.1, f32[2,256,2048]{2,1,0:T(8,128)} %beams.1, s32[2]{0:T(128)} %row_block_in.1, s32[2]{0:T(128)} %col_block_in.1, s32[2,2]{1,0:T(2,128)} %band_in.1, f32[2]{0:T(128)} %row_frac_in.1, f32[2]{0:T(128)} %col_frac_in.1), custom_call_target="tpu_custom_call" | custom-call | tf_op jit(solution)/shard_map/pallas_call | solution.py:491
  58.0 0.9 %shard_map.95 = (f32[512,128]{1,0:T(8,128)}, f32[512,128]{1,0:T(8,128)}, f32[512,128]{1,0:T(8,128)}) custom-call(f32[512,128]{1,0:T(8,128)S(1)} %get-tuple-element.6.numer, f32[512,128]{1,0:T(8,128)S(1)} %get-tuple-element.7.weight, f32[512,128]{1,0:T(8,128)S(1)} %get-tuple-element.8.normalised), custom_call_target="tpu_custom_call" | custom-call | tf_op jit(solution)/shard_map/pallas_call | solution.py:536

commit v5 on v4

--- a/solution.py
+++ b/solution.py
@@ -14,7 +14,7 @@
 UNROLL = 2
 SKY = 512
 SEND_SLOTS, RECV_SLOTS = (4, 4, 4, 4), (8, 8, 8)
-LAG_B, LAG_C, LAG_D, LAG_F = 3, 6, 9, 12
+LAG_B, LAG_C, LAG_D, LAG_F = 3, 6, 8, 11
 
 
 def kernel(

time: 59.1 us -> 59.5 us (level)
  no operation moved by 1% of the time
where the time goes in v5:
time: 59.5 us; the launch traced here: 59.4 us
  Pallas kernels  58.8 us (99%)
  between operations  0.64 us (1%)
    pallas_call x1, Pallas kernels, body(): pl.pallas_call(kernel, out_shape=(pltpu.VMEM((SKY, 128), f32),) * 3, in_s...  57.9 us

profile of v5, /device:TPU:1, one launch (start us, length us, event | category | flops | bytes accessed | tf_op | source)
XLA Modules:
  0.0 59.4 jit_solution(12303834347980850680)
XLA Ops:
  0.6 57.9 %shard_map.94 = (f32[512,128]{1,0:T(8,128)S(1)}, f32[512,128]{1,0:T(8,128)S(1)}, f32[512,128]{1,0:T(8,128)S(1)}) custom-call(f32[2,256,2048]{2,1,0:T(8,128)} %images.1, f32[2,256,2048]{2,1,0:T(8,128)} %beams.1, s32[2]{0:T(128)} %row_block_in.1, s32[2]{0:T(128)} %col_block_in.1, s32[2,2]{1,0:T(2,128)} %band_in.1, f32[2]{0:T(128)} %row_frac_in.1, f32[2]{0:T(128)} %col_frac_in.1), custom_call_target="tpu_custom_call" | custom-call | tf_op jit(solution)/shard_map/pallas_call | solution.py:491
  58.5 0.9 %shard_map.95 = (f32[512,128]{1,0:T(8,128)}, f32[512,128]{1,0:T(8,128)}, f32[512,128]{1,0:T(8,128)}) custom-call(f32[512,128]{1,0:T(8,128)S(1)} %get-tuple-element.6.numer, f32[512,128]{1,0:T(8,128)S(1)} %get-tuple-element.7.weight, f32[512,128]{1,0:T(8,128)S(1)} %get-tuple-element.8.normalised), custom_call_target="tpu_custom_call" | custom-call | tf_op jit(solution)/shard_map/pallas_call | solution.py:536
